TPU v7x, 32 devices: a whole 2x2x4 slice. The times are simulated.
32 devices in a mesh: fsdp: 4 (over y, core), sp: 8 (over z, x).
Axes of the slice: x: 2, y: 2, z: 4, core: 2. Of those that a mesh axis runs over, the one named last changes fastest.
Arguments:
- hidden: bfloat16 [2048, 8192], P('sp', 'fsdp'), may hold values from -23 to 23
- w_query: bfloat16 [8192, 1024], P('fsdp', 'sp'), may hold values from -0.125 to 0.125
- w_keyvalue: bfloat16 [8192, 256], P('fsdp', 'sp'), may hold values from -0.125 to 0.125
- w_output: bfloat16 [1024, 8192], P('sp', 'fsdp'), may hold values from -0.75 to 0.75
- segment_ids: int32 [2048], P('sp'), may hold values from 0 to 7, never falling along the last dimension, each value on 1 to 512 neighbouring positions
Outputs:
- attended: bfloat16 [2048, 8192], P('sp', 'fsdp')
Inputs may be any that keep to these rules, and one draw needn't show every extreme that they name: `segment_ids`: segment ids never fall along the sequence; every episode has between 1 and 512 tokens.
All inputs are finite; a program needn't handle non-finite values.
Results may differ from a plain program's by a relative error of at most 0.0085.
The roundings to bfloat16 on the way count: a program that leaves them out, or rounds other values in their place, can miss the bound.
Values may be sent and summed in bfloat16 or wider, within the bound.
A program may use at most 128 MiB of HBM per device.

v0:
```python
import math
import jax
import jax.numpy as jnp
from jax import lax
from jax.sharding import PartitionSpec as P

HD = 128
GROUP = 8
ROPE_BASE = 500000.0
NEG_FILL = -1e30


def rotate(values, positions, head_count, width):
    row_count = values.shape[0]
    shaped = values.reshape(row_count, head_count, width)
    half_width = width // 2
    frequency = jnp.exp(
        jnp.arange(half_width, dtype=jnp.float32) * (-2.0 * math.log(ROPE_BASE) / width)
    )
    angles = positions.astype(jnp.float32)[:, None] * frequency[None, :]
    cosine = jnp.cos(angles)[:, None, :]
    sine_part = jnp.sin(angles)[:, None, :]
    lower_half = shaped[:, :, :half_width]
    upper_half = shaped[:, :, half_width:]
    turned = jnp.concatenate(
        [
            lower_half * cosine - upper_half * sine_part,
            upper_half * cosine + lower_half * sine_part,
        ],
        axis=2,
    )
    return turned.reshape(row_count, head_count * width)


def split_keys(kv_sum, positions, kv_count, width):
    row_count = kv_sum.shape[0]
    shaped = kv_sum.reshape(row_count, kv_count, 2, width)
    key_part = rotate(
        shaped[:, :, 0, :].reshape(row_count, kv_count * width), positions, kv_count, width
    )
    key_part = key_part.reshape(row_count, kv_count, 1, width)
    return jnp.concatenate([key_part, shaped[:, :, 1:2, :]], axis=2).astype(jnp.bfloat16)


def merge_keys(
    state_in, query_tile, query_pos_tile, query_seg_tile, key_tile, key_pos_tile, key_seg_tile
):
    running_max, running_sum, weighted = state_in
    allowed = (key_pos_tile[None, :] <= query_pos_tile[:, None]) & (
        key_seg_tile[None, :] == query_seg_tile[:, None]
    )
    key_part = key_tile[:, :HD]
    value_part = key_tile[:, HD:]
    scores = lax.dot_general(
        query_tile, key_part, (((1,), (1,)), ((), ())), preferred_element_type=jnp.float32
    ) * HD ** (-0.5)
    masked = jnp.where(allowed, scores, NEG_FILL)
    new_max = jnp.maximum(running_max, jnp.max(masked, axis=1))
    weights = jnp.where(allowed, jnp.exp(masked - new_max[:, None]), 0.0)
    new_sum = jnp.sum(weights, axis=1)
    new_weighted = jnp.dot(
        weights.astype(jnp.bfloat16), value_part, preferred_element_type=jnp.float32
    )
    return (new_max, new_sum, new_weighted)


def on_device(hidden, w_query, w_keyvalue, w_output, segment_ids):
    fsdp_count = lax.axis_size("fsdp")
    seq_count = lax.axis_size("sp")
    fsdp_index = lax.axis_index("fsdp")
    seq_index = lax.axis_index("sp")
    tok_rows = hidden.shape[0]
    sub_rows = tok_rows // fsdp_count
    kv_count = seq_count // GROUP
    query_rows = seq_count * sub_rows
    offsets = jnp.arange(query_rows, dtype=jnp.int32)
    query_pos = offsets // sub_rows * tok_rows + fsdp_index * sub_rows + offsets % sub_rows
    own_positions = (
        seq_index * tok_rows + fsdp_index * sub_rows + jnp.arange(sub_rows, dtype=jnp.int32)
    )

    def project(weight_block):
        return jnp.dot(hidden, weight_block, preferred_element_type=jnp.float32)

    query_part = project(lax.all_gather(w_query, "sp", axis=1, tiled=True))
    kv_part = project(lax.all_gather(w_keyvalue, "sp", axis=1, tiled=True))
    query_sum, kv_sum = (
        lax.psum_scatter(query_part, "fsdp", scatter_dimension=0, tiled=True),
        lax.psum_scatter(kv_part, "fsdp", scatter_dimension=0, tiled=True),
    )
    query_local = rotate(query_sum, own_positions, seq_count, HD).astype(jnp.bfloat16)
    pairs = split_keys(kv_sum, own_positions, kv_count, HD)
    expanded = jnp.repeat(pairs, GROUP, axis=1).reshape(sub_rows, seq_count * 2 * HD)
    query_head, kv_head = (
        lax.all_to_all(query_local, "sp", split_axis=1, concat_axis=0, tiled=True),
        lax.all_to_all(expanded, "sp", split_axis=1, concat_axis=0, tiled=True),
    )
    segment_all = lax.all_gather(segment_ids, "sp", axis=0, tiled=True)
    query_seg = segment_all[query_pos]
    initial = (
        jnp.full((query_rows,), NEG_FILL, jnp.float32),
        jnp.zeros((query_rows,), jnp.float32),
        jnp.zeros((query_rows, HD), jnp.float32),
    )
    block_keys = lax.all_gather(kv_head, "fsdp", axis=0, tiled=True)
    piece_rows = block_keys.shape[0]
    row_ids = jnp.arange(piece_rows, dtype=jnp.int32)
    source_id = row_ids // query_rows
    within = row_ids % query_rows
    key_pos = within // sub_rows * tok_rows + source_id * sub_rows + within % sub_rows
    key_seg = segment_all[key_pos]
    final_max, final_sum, final_weighted = merge_keys(
        initial, query_head, query_pos, query_seg, block_keys, key_pos, key_seg
    )
    attention = (final_weighted / final_sum[:, None]).astype(jnp.bfloat16)
    back_rows = lax.all_to_all(attention, "sp", split_axis=0, concat_axis=1, tiled=True)
    mixed_rows = lax.all_gather(back_rows, "fsdp", axis=0, tiled=True)
    result = jnp.dot(
        mixed_rows,
        lax.all_gather(w_output, "sp", axis=0, tiled=True),
        preferred_element_type=jnp.float32,
    )
    return result.astype(jnp.bfloat16)


def solution(mesh):
    in_specs = (P("sp", "fsdp"), P("fsdp", "sp"), P("fsdp", "sp"), P("sp", "fsdp"), P("sp"))
    out_specs = P("sp", "fsdp")
    return jax.shard_map(
        on_device, mesh=mesh, in_specs=in_specs, out_specs=out_specs, check_vma=False
    )
```

profile of v0, /device:TPU:0, one launch (start us, length us, event | category | flops | bytes accessed | tf_op | source)
XLA Modules:
  0.0 280.8 jit_solution(3011996384781910842)
XLA Ops:
  6.5 0.0 copy-start
  6.5 0.0 all-gather.8.cloned.1.call-start
  6.5 0.7 all-gather.8.cloned.1.call-update
  7.3 0.0 all-gather.6.cloned.1.call-start
  7.3 0.7 all-gather.6.cloned.1.call-update
  8.0 0.0 reduce-scatter.5.cloned.1.call-start
  8.1 44.4 %all-gather.8.cloned.1.call-done = bf16[2048,256]{0,1:T(8,128)(2,1)} async-done(((bf16[2048,32]{0,1:T(8,128)(2,1)}), bf16[2048,256]{0,1:T(8,128)(2,1)}) %all-gather.8.cloned.1.call-update) | async-done | bytes 1048592 | tf_op jit(solution)/shard_map/all_gather | solution.py:86
  52.5 0.0 copy-done
  52.5 2.4 fusion.62
  54.9 0.0 reduce-scatter.5.cloned.1.call-update
  54.9 0.0 reduce-scatter.3.cloned.1.call-start
  55.0 72.9 %all-gather.6.cloned.1.call-done = bf16[2048,1024]{1,0:T(8,128)(2,1)} async-done(((bf16[2048,128]{1,0:T(8,128)(2,1)}), bf16[2048,1024]{1,0:T(8,128)(2,1)}) %all-gather.6.cloned.1.call-update) | async-done | bytes 4194320 | tf_op jit(solution)/shard_map/all_gather | solution.py:85
  127.9 4.4 %fusion.61 = f32[256,1024]{1,0:T(8,128)} fusion(bf16[256,2048]{1,0:T(8,128)(2,1)S(1)} %copy-done, bf16[2048,1024]{1,0:T(8,128)(2,1)} %all-gather.6.cloned.1.call-done), kind=kOutput, calls=%fused_computation.109 | convolution fusion | flops 1073741824 | bytes 6291456 | tf_op jit(solution)/shard_map/dot_general | solution.py:83
  132.3 0.0 copy-start.1
  132.3 0.0 reduce-scatter.3.cloned.1.call-update
  132.3 0.0 all-gather.10.cloned.1.call-start
  132.4 16.3 %reduce-scatter.5.cloned.1.call-done = f32[64,256]{1,0:T(8,128)} async-done(((f32[256,256]{1,0:T(8,128)}), f32[64,256]{1,0:T(8,128)}) %reduce-scatter.5.cloned.1.call-update) | async-done | bytes 65552 | tf_op jit(solution)/shard_map/reduce_scatter | solution.py:89
  148.7 0.9 reshape.398
  149.7 0.2 fusion.19
  149.9 0.1 copy_bitcast_fusion.1
  150.0 14.1 %all_to_all.51 = bf16[64,8,256]{2,0,1:T(8,128)(2,1)} all-to-all(bf16[64,8,256]{2,0,1:T(8,128)(2,1)S(1)} %broadcast_in_dim.10), channel_id=1, replica_groups=mesh['fsdp'=4,'sp'=8] {'sp'}, dimensions={1} | all-to-all | bytes 524288 | tf_op jit(solution)/shard_map/all_to_all | solution.py:96
  164.1 0.0 all-gather.10.cloned.1.call-update
  164.1 0.0 all-gather.12.cloned.1.call-start
  164.1 0.5 all-gather.12.cloned.1.call-update
  164.7 0.2 multiply_cosine_fusion.1
  164.9 11.0 %reduce-scatter.3.cloned.1.call-done = f32[64,1024]{1,0:T(8,128)} async-done(((f32[256,1024]{1,0:T(8,128)}), f32[64,1024]{1,0:T(8,128)}) %reduce-scatter.3.cloned.1.call-update) | async-done | bytes 262160 | tf_op jit(solution)/shard_map/reduce_scatter | solution.py:88
  175.9 1.0 copy.25
  176.9 0.1 fusion.60
  177.0 0.1 subtract_convert_fusion
  177.2 0.8 pad_maximum_fusion
  177.9 5.5 %all-to-all-start = ((bf16[64,8,128]{2,0,1:T(8,128)(2,1)}), bf16[64,8,128]{2,0,1:T(8,128)(2,1)S(1)}, u32[]{:S(2)}, u32[]{:S(2)}) async-start(bf16[64,8,128]{2,0,1:T(8,128)(2,1)} %pad_maximum_fusion), calls=%async_computation.1 | async-start | bytes 262144 | tf_op jit(solution)/shard_map/all_to_all | solution.py:95
  183.4 0.0 copy-done.1
  183.5 21.0 %all-gather = s32[8,1,256]{2,1,0:T(1,128)S(1)} all-gather(s32[1,1,256]{2,1,0:T(1,128)S(1)} %bitcast.48), channel_id=1, replica_groups=mesh['fsdp'=4,'sp'=8] {'sp'}, dimensions={0}, use_global_device_ids=true | all-gather | bytes 9216 | tf_op jit(solution)/shard_map/all_gather | solution.py:98
  204.5 3.1 %gather_fusion.1 = s32[512]{0:T(512)S(1)} fusion(s32[2048]{0:T(1024)S(1)} %bitcast.37, s32[1024]{0:T(1024)S(1)} %pad_clamp_fusion), kind=kCustom, calls=%fused_computation.1 | custom fusion | bytes 6144 | tf_op jit(solution)/shard_map/gather | solution.py:99
  207.6 11.8 %gather_fusion = s32[2048]{0:T(1024)S(1)} fusion(s32[2048]{0:T(1024)S(1)} %bitcast.38, s32[2048]{0:T(1024)S(1)} %broadcast_clamp_fusion), kind=kCustom, calls=%fused_computation | custom fusion | bytes 24576 | tf_op jit(solution)/shard_map/gather | solution.py:111
  219.4 0.0 all-gather.10.cloned.1.call-done
  219.5 0.0 all-to-all-done
  219.5 0.0 copy-start.2
  219.5 2.4 fusion
  221.8 1.7 fusion.1
  223.5 0.0 copy-done.2
  223.5 1.3 fusion.8
  224.8 9.8 %all_to_all.52 = bf16[8,64,128]{2,1,0:T(8,128)(2,1)S(1)} all-to-all(bf16[8,64,128]{2,1,0:T(8,128)(2,1)S(1)} %bitcast.44), channel_id=1, replica_groups=mesh['fsdp'=4,'sp'=8] {'sp'}, dimensions={0} | all-to-all | bytes 262144 | tf_op jit(solution)/shard_map/all_to_all | solution.py:116
  234.7 6.5 %all_gather.22 = bf16[256,1024]{1,0:T(8,128)(2,1)S(1)} all-gather(bf16[64,1024]{1,0:T(8,128)(2,1)S(1)} %copy_bitcast_fusion), channel_id=1, replica_groups=mesh['fsdp'=4,'sp'=8] {'fsdp'}, dimensions={0}, use_global_device_ids=true | all-gather | bytes 655360 | tf_op jit(solution)/shard_map/all_gather | solution.py:117
  241.2 28.3 %all-gather.12.cloned.1.call-done = bf16[1024,2048]{1,0:T(8,128)(2,1)} async-done(((bf16[128,2048]{1,0:T(8,128)(2,1)}), bf16[1024,2048]{1,0:T(8,128)(2,1)}) %all-gather.12.cloned.1.call-update) | async-done | bytes 4194320 | tf_op jit(solution)/shard_map/all_gather | solution.py:120
  269.5 4.4 %convolution_convert_fusion = bf16[256,2048]{1,0:T(8,128)(2,1)} fusion(bf16[256,1024]{1,0:T(8,128)(2,1)S(1)} %all_gather.22, bf16[1024,2048]{1,0:T(8,128)(2,1)} %all-gather.12.cloned.1.call-done), kind=kOutput, calls=%fused_computation.6 | convolution fusion | flops 1074266112 | bytes 5767168 | tf_op jit(solution)/shard_map/dot_general | solution.py:118
  (15 shorter events, 0.2 us)
Async XLA Ops:
  6.5 46.0 %copy-start = (bf16[256,2048]{1,0:T(8,128)(2,1)S(1)}, bf16[256,2048]{1,0:T(8,128)(2,1)}, u32[]{:S(2)}) copy-start(bf16[256,2048]{1,0:T(8,128)(2,1)} %param.5) | copy-start | bytes 3145732
  6.5 46.0 %all-gather.8.cloned.1.call-start = ((), (), s32[]{:S(2)}) async-start(), calls=%async_computation.7 | async-start | bytes 1179648 | tf_op jit(solution)/shard_map/all_gather | solution.py:86
  7.3 120.7 %all-gather.6.cloned.1.call-start = ((), (), s32[]{:S(2)}) async-start(), calls=%async_computation.5 | async-start | bytes 4718592 | tf_op jit(solution)/shard_map/all_gather | solution.py:85
  8.0 140.7 %reduce-scatter.5.cloned.1.call-start = ((), (), s32[]{:S(2)}) async-start(), calls=%async_computation.8 | async-start | bytes 327680 | tf_op jit(solution)/shard_map/reduce_scatter | solution.py:89
  54.9 121.0 %reduce-scatter.3.cloned.1.call-start = ((), (), s32[]{:S(2)}) async-start(), calls=%async_computation.6 | async-start | bytes 1310720 | tf_op jit(solution)/shard_map/reduce_scatter | solution.py:88
  132.3 51.1 %copy-start.1 = (s32[256]{0:T(256)S(1)}, s32[256]{0:T(256)}, u32[]{:S(2)}) copy-start(s32[256]{0:T(256)} %param.9) | copy-start | bytes 3076
  132.3 87.1 %all-gather.10.cloned.1.call-start = ((), (), s32[]{:S(2)}) async-start(), calls=%async_computation.9 | async-start | bytes 1310720 | tf_op jit(solution)/shard_map/all_gather | solution.py:105
  164.1 105.4 %all-gather.12.cloned.1.call-start = ((), (), s32[]{:S(2)}) async-start(), calls=%async_computation.10 | async-start | bytes 4718592 | tf_op jit(solution)/shard_map/all_gather | solution.py:120
  177.9 41.5 %all-to-all-start = ((bf16[64,8,128]{2,0,1:T(8,128)(2,1)}), bf16[64,8,128]{2,0,1:T(8,128)(2,1)S(1)}, u32[]{:S(2)}, u32[]{:S(2)}) async-start(bf16[64,8,128]{2,0,1:T(8,128)(2,1)} %pad_maximum_fusion), calls=%async_computation.1 | async-start | bytes 262144 | tf_op jit(solution)/shard_map/all_to_all | solution.py:95
  219.5 4.1 %copy-start.2 = (bf16[2048,256]{1,0:T(8,128)(2,1)S(1)}, bf16[2048,256]{1,0:T(8,128)(2,1)}, u32[]{:S(2)}) copy-start(bf16[2048,256]{1,0:T(8,128)(2,1)} %all-gather.10.cloned.1.call-done) | copy-start | bytes 3145732
Sparse Core Ops, SparseCore 0:
  9.5 42.9 all-gather.7
  54.5 73.3 all-gather.5
  130.4 18.2 reduce-scatter.4
  151.1 24.8 reduce-scatter.2
  177.3 16.6 all-gather.9
  196.0 73.3 all-gather.11
where the time goes:
time: 281 us
  waiting for transfers between devices  175 us (62%)
  blocking collectives  51.4 us (18%)
  local copies, waits for them, and re-layouts  17 us (6%)
  matrix products  14.9 us (5%)
  between operations  13.7 us (5%)
  starting transfers between devices  5.72 us (2%)
  other arithmetic  3.14 us (1%)
    all_gather x1, waiting for transfers between devices, on_device(): query_part = project(lax.all_gather(w_query, 'sp', axis=1, tiled=True))  72.9 us
    all_gather x1, waiting for transfers between devices, on_device(): kv_part = project(lax.all_gather(w_keyvalue, 'sp', axis=1, tiled=True))  44.4 us
    all_gather x1, waiting for transfers between devices, on_device(): lax.all_gather(w_output, 'sp', axis=0, tiled=True)  28.3 us
    all_gather x1, blocking collectives, on_device(): segment_all = lax.all_gather(segment_ids, 'sp', axis=0, tiled=True)  21 us
    reduce_scatter x1, waiting for transfers between devices, on_device(): lax.psum_scatter(kv_part, 'fsdp', scatter_dimension=0, tiled=True)  16.3 us
    all_to_all x1, blocking collectives, on_device(): lax.all_to_all(expanded, 'sp', split_axis=1, concat_axis=0, tiled=True)  14.1 us
    gather x1, local copies, waits for them, and re-layouts, on_device(): key_seg = segment_all[key_pos]  11.8 us
    reduce_scatter x1, waiting for transfers between devices, on_device(): lax.psum_scatter(query_part, 'fsdp', scatter_dimension=0, tiled=True)  11 us
  transfers between devices with their start and end apart: 7, of which 5 were waited for; matrix products, arithmetic and copies ran while one was open for 11% of the time, Pallas kernels for 0%

commit v1 on v0

--- a/solution.py
+++ b/solution.py
@@ -95,7 +95,12 @@
         lax.all_to_all(query_local, "sp", split_axis=1, concat_axis=0, tiled=True),
         lax.all_to_all(expanded, "sp", split_axis=1, concat_axis=0, tiled=True),
     )
-    segment_all = lax.all_gather(segment_ids, "sp", axis=0, tiled=True)
+    ring = [segment_ids]
+    for hop in range(7):
+        ring.append(lax.ppermute(ring[-1], "sp", [(dev, (dev + 1) % 8) for dev in range(8)]))
+    segment_all = jnp.roll(
+        jnp.concatenate(ring[::-1], axis=0), (lax.axis_index("sp") + 1) * ring[0].shape[0], axis=0
+    )
     query_seg = segment_all[query_pos]
     initial = (
         jnp.full((query_rows,), NEG_FILL, jnp.float32),

time: 281 us -> 283 us (level)
  waiting for transfers between devices: 175 us -> 193 us
  blocking collectives: 51.4 us -> 35.9 us
    ppermute x0 -> x7, waiting for transfers between devices: none -> 42.3 us  [on_device(): lax.ppermute(ring[-1], 'sp', [(dev, (dev + 1) % 8) for dev in range(8)])]
    all_gather x1 -> x0, blocking collectives: 21 us -> none  [on_device(): segment_all = lax.all_gather(segment_ids, 'sp', axis=0, tiled=True)]
    all_gather x1, waiting for transfers between devices: 28.3 us -> 15 us  [on_device(): lax.all_gather(w_output, 'sp', axis=0, tiled=True)]
    reduce_scatter x1, waiting for transfers between devices: 11 us -> 0.02 us  [on_device(): lax.psum_scatter(query_part, 'fsdp', scatter_dimension=0, tiled=True)]
    all_to_all x1, blocking collectives: 9.84 us -> 15 us  [on_device(): lax.all_to_all(attention, 'sp', split_axis=0, concat_axis=1, tiled=True)]
  transfers between devices with their start and end apart: 7 -> 14, of which waited for: 5 -> 11; matrix products, arithmetic and copies ran while one was open for 11% -> 11% of each run, Pallas kernels for 0% -> 0%
where the time goes in v1:
time: 283 us
  waiting for transfers between devices  193 us (68%)
  blocking collectives  35.9 us (13%)
  local copies, waits for them, and re-layouts  17.2 us (6%)
  matrix products  14.9 us (5%)
  between operations  13.8 us (5%)
  starting transfers between devices  5.06 us (2%)
  other arithmetic  3.14 us (1%)
    all_gather x1, waiting for transfers between devices, on_device(): query_part = project(lax.all_gather(w_query, 'sp', axis=1, tiled=True))  72.9 us
    all_gather x1, waiting for transfers between devices, on_device(): kv_part = project(lax.all_gather(w_keyvalue, 'sp', axis=1, tiled=True))  44.4 us
    ppermute x7, waiting for transfers between devices, on_device(): lax.ppermute(ring[-1], 'sp', [(dev, (dev + 1) % 8) for dev in range(8)])  42.3 us
    reduce_scatter x1, waiting for transfers between devices, on_device(): lax.psum_scatter(kv_part, 'fsdp', scatter_dimension=0, tiled=True)  16.3 us
    all_gather x1, waiting for transfers between devices, on_device(): lax.all_gather(w_output, 'sp', axis=0, tiled=True)  15 us
    all_to_all x1, blocking collectives, on_device(): lax.all_to_all(attention, 'sp', split_axis=0, concat_axis=1, tiled=True)  15 us
    all_to_all x1, blocking collectives, on_device(): lax.all_to_all(expanded, 'sp', split_axis=1, concat_axis=0, tiled=True)  14.1 us
    gather x1, local copies, waits for them, and re-layouts, on_device(): key_seg = segment_all[key_pos]  11.8 us
  transfers between devices with their start and end apart: 14, of which 11 were waited for; matrix products, arithmetic and copies ran while one was open for 11% of the time, Pallas kernels for 0%

profile of v1, /device:TPU:0, one launch (start us, length us, event | category | flops | bytes accessed | tf_op | source)
XLA Modules:
  0.0 282.9 jit_solution(9061377041045727111)
XLA Ops:
  6.5 0.0 copy-start
  6.5 0.0 all-gather.7.cloned.1.call-start
  6.5 0.7 all-gather.7.cloned.1.call-update
  7.3 0.0 all-gather.5.cloned.1.call-start
  7.3 0.7 all-gather.5.cloned.1.call-update
  8.0 0.0 reduce-scatter.5.cloned.1.call-start
  8.1 44.4 %all-gather.7.cloned.1.call-done = bf16[2048,256]{0,1:T(8,128)(2,1)} async-done(((bf16[2048,32]{0,1:T(8,128)(2,1)}), bf16[2048,256]{0,1:T(8,128)(2,1)}) %all-gather.7.cloned.1.call-update) | async-done | bytes 1048592 | tf_op jit(solution)/shard_map/all_gather | solution.py:86
  52.5 0.0 copy-done
  52.5 2.4 fusion.62
  54.9 0.0 reduce-scatter.5.cloned.1.call-update
  54.9 0.0 copy-start.1
  54.9 0.0 reduce-scatter.3.cloned.1.call-start
  55.0 72.9 %all-gather.5.cloned.1.call-done = bf16[2048,1024]{1,0:T(8,128)(2,1)} async-done(((bf16[2048,128]{1,0:T(8,128)(2,1)}), bf16[2048,1024]{1,0:T(8,128)(2,1)}) %all-gather.5.cloned.1.call-update) | async-done | bytes 4194320 | tf_op jit(solution)/shard_map/all_gather | solution.py:85
  127.9 4.4 %fusion.61 = f32[256,1024]{1,0:T(8,128)} fusion(bf16[256,2048]{1,0:T(8,128)(2,1)S(1)} %copy-done, bf16[2048,1024]{1,0:T(8,128)(2,1)} %all-gather.5.cloned.1.call-done), kind=kOutput, calls=%fused_computation.125 | convolution fusion | flops 1073741824 | bytes 6291456 | tf_op jit(solution)/shard_map/dot_general | solution.py:83
  132.3 0.0 reduce-scatter.3.cloned.1.call-update
  132.3 0.0 all-gather.9.cloned.1.call-start
  132.4 16.3 %reduce-scatter.5.cloned.1.call-done = f32[64,256]{1,0:T(8,128)} async-done(((f32[256,256]{1,0:T(8,128)}), f32[64,256]{1,0:T(8,128)}) %reduce-scatter.5.cloned.1.call-update) | async-done | bytes 65552 | tf_op jit(solution)/shard_map/reduce_scatter | solution.py:89
  148.7 0.9 reshape.398
  149.7 0.2 fusion.19
  149.9 0.1 copy_bitcast_fusion.1
  150.0 14.1 %all_to_all.51 = bf16[64,8,256]{2,0,1:T(8,128)(2,1)} all-to-all(bf16[64,8,256]{2,0,1:T(8,128)(2,1)S(1)} %broadcast_in_dim.10), channel_id=1, replica_groups=mesh['fsdp'=4,'sp'=8] {'sp'}, dimensions={1} | all-to-all | bytes 524288 | tf_op jit(solution)/shard_map/all_to_all | solution.py:96
  164.1 0.0 all-gather.9.cloned.1.call-update
  164.1 0.0 all-gather.11.cloned.1.call-start
  164.1 0.5 all-gather.11.cloned.1.call-update
  164.7 0.0 copy-done.1
  164.7 1.5 collective-permute-start
  166.1 0.2 multiply_cosine_fusion.1
  166.4 4.6 %collective-permute-done = s32[256]{0:T(256)S(1)} collective-permute-done((s32[256]{0:T(256)S(1)}, s32[256]{0:T(256)S(1)}, u32[]{:S(2)}, u32[]{:S(2)}) %collective-permute-start) | collective-permute-done | bytes 1056 | tf_op jit(solution)/shard_map/ppermute | solution.py:100
  171.0 0.0 collective-permute-start.1
  171.0 6.3 %collective-permute-done.1 = s32[256]{0:T(256)S(1)} collective-permute-done((s32[256]{0:T(256)S(1)}, s32[256]{0:T(256)S(1)}, u32[]{:S(2)}, u32[]{:S(2)}) %collective-permute-start.1) | collective-permute-done | bytes 1056 | tf_op jit(solution)/shard_map/ppermute | solution.py:100
  177.3 0.0 collective-permute-start.2
  177.3 6.3 %collective-permute-done.2 = s32[256]{0:T(256)S(1)} collective-permute-done((s32[256]{0:T(256)S(1)}, s32[256]{0:T(256)S(1)}, u32[]{:S(2)}, u32[]{:S(2)}) %collective-permute-start.2) | collective-permute-done | bytes 1056 | tf_op jit(solution)/shard_map/ppermute | solution.py:100
  183.5 0.0 collective-permute-start.3
  183.6 6.3 %collective-permute-done.3 = s32[256]{0:T(256)S(1)} collective-permute-done((s32[256]{0:T(256)S(1)}, s32[256]{0:T(256)S(1)}, u32[]{:S(2)}, u32[]{:S(2)}) %collective-permute-start.3) | collective-permute-done | bytes 1056 | tf_op jit(solution)/shard_map/ppermute | solution.py:100
  189.8 0.0 collective-permute-start.4
  189.8 6.3 %collective-permute-done.4 = s32[256]{0:T(256)S(1)} collective-permute-done((s32[256]{0:T(256)S(1)}, s32[256]{0:T(256)S(1)}, u32[]{:S(2)}, u32[]{:S(2)}) %collective-permute-start.4) | collective-permute-done | bytes 1056 | tf_op jit(solution)/shard_map/ppermute | solution.py:100
  196.1 0.0 collective-permute-start.5
  196.1 6.3 %collective-permute-done.5 = s32[256]{0:T(256)S(1)} collective-permute-done((s32[256]{0:T(256)S(1)}, s32[256]{0:T(256)S(1)}, u32[]{:S(2)}, u32[]{:S(2)}) %collective-permute-start.5) | collective-permute-done | bytes 1056 | tf_op jit(solution)/shard_map/ppermute | solution.py:100
  202.4 0.0 collective-permute-start.6
  202.4 6.4 %collective-permute-done.6 = s32[256]{0:T(256)S(1)} collective-permute-done((s32[256]{0:T(256)S(1)}, s32[256]{0:T(256)S(1)}, u32[]{:S(2)}, u32[]{:S(2)}) %collective-permute-start.6) | collective-permute-done | bytes 1056 | tf_op jit(solution)/shard_map/ppermute | solution.py:100
  208.9 0.0 reduce-scatter.3.cloned.1.call-done
  208.9 1.0 copy.25
  209.9 0.1 fusion.60
  210.1 0.1 subtract_convert_fusion
  210.2 0.8 pad_maximum_fusion
  210.9 3.4 %all-to-all-start = ((bf16[64,8,128]{2,0,1:T(8,128)(2,1)}), bf16[64,8,128]{2,0,1:T(8,128)(2,1)S(1)}, u32[]{:S(2)}, u32[]{:S(2)}) async-start(bf16[64,8,128]{2,0,1:T(8,128)(2,1)} %pad_maximum_fusion), calls=%async_computation.1 | async-start | bytes 262144 | tf_op jit(solution)/shard_map/all_to_all | solution.py:95
  214.4 0.1 dynamic_slice.4
  214.5 11.8 %gather_fusion = s32[2048]{0:T(1024)S(1)} fusion(s32[2048]{0:T(1024)S(1)} %dynamic_slice.4, s32[2048]{0:T(1024)S(1)} %broadcast_clamp_fusion), kind=kCustom, calls=%fused_computation | custom fusion | bytes 24576 | tf_op jit(solution)/shard_map/gather | solution.py:116
  226.2 3.1 %gather_fusion.1 = s32[512]{0:T(512)S(1)} fusion(s32[2048]{0:T(1024)S(1)} %dynamic_slice.4, s32[1024]{0:T(1024)S(1)} %pad_clamp_fusion), kind=kCustom, calls=%fused_computation.1 | custom fusion | bytes 6144 | tf_op jit(solution)/shard_map/gather | solution.py:104
  229.4 0.0 all-gather.9.cloned.1.call-done
  229.4 0.0 all-to-all-done
  229.4 0.0 copy-start.2
  229.4 2.4 fusion
  231.8 1.7 fusion.1
  233.5 0.0 copy-done.2
  233.5 1.3 fusion.8
  234.8 15.0 %all_to_all.52 = bf16[8,64,128]{2,1,0:T(8,128)(2,1)S(1)} all-to-all(bf16[8,64,128]{2,1,0:T(8,128)(2,1)S(1)} %bitcast.40), channel_id=1, replica_groups=mesh['fsdp'=4,'sp'=8] {'sp'}, dimensions={0} | all-to-all | bytes 262144 | tf_op jit(solution)/shard_map/all_to_all | solution.py:121
  249.8 6.8 %all_gather.18 = bf16[256,1024]{1,0:T(8,128)(2,1)S(1)} all-gather(bf16[64,1024]{1,0:T(8,128)(2,1)S(1)} %copy_bitcast_fusion), channel_id=1, replica_groups=mesh['fsdp'=4,'sp'=8] {'fsdp'}, dimensions={0}, use_global_device_ids=true | all-gather | bytes 655360 | tf_op jit(solution)/shard_map/all_gather | solution.py:122
  256.6 15.0 %all-gather.11.cloned.1.call-done = bf16[1024,2048]{1,0:T(8,128)(2,1)} async-done(((bf16[128,2048]{1,0:T(8,128)(2,1)}), bf16[1024,2048]{1,0:T(8,128)(2,1)}) %all-gather.11.cloned.1.call-update) | async-done | bytes 4194320 | tf_op jit(solution)/shard_map/all_gather | solution.py:125
  271.6 4.4 %convolution_convert_fusion = bf16[256,2048]{1,0:T(8,128)(2,1)} fusion(bf16[256,1024]{1,0:T(8,128)(2,1)S(1)} %all_gather.18, bf16[1024,2048]{1,0:T(8,128)(2,1)} %all-gather.11.cloned.1.call-done), kind=kOutput, calls=%fused_computation.6 | convolution fusion | flops 1074266112 | bytes 5767168 | tf_op jit(solution)/shard_map/dot_general | solution.py:123
  (32 shorter events, 0.3 us)
Async XLA Ops:
  6.5 46.0 %copy-start = (bf16[256,2048]{1,0:T(8,128)(2,1)S(1)}, bf16[256,2048]{1,0:T(8,128)(2,1)}, u32[]{:S(2)}) copy-start(bf16[256,2048]{1,0:T(8,128)(2,1)} %param.5) | copy-start | bytes 3145732
  6.5 46.0 %all-gather.7.cloned.1.call-start = ((), (), s32[]{:S(2)}) async-start(), calls=%async_computation.7 | async-start | bytes 1179648 | tf_op jit(solution)/shard_map/all_gather | solution.py:86
  7.3 120.7 %all-gather.5.cloned.1.call-start = ((), (), s32[]{:S(2)}) async-start(), calls=%async_computation.5 | async-start | bytes 4718592 | tf_op jit(solution)/shard_map/all_gather | solution.py:85
  8.0 140.7 %reduce-scatter.5.cloned.1.call-start = ((), (), s32[]{:S(2)}) async-start(), calls=%async_computation.8 | async-start | bytes 327680 | tf_op jit(solution)/shard_map/reduce_scatter | solution.py:89
  54.9 109.8 %copy-start.1 = (s32[256]{0:T(256)S(1)}, s32[256]{0:T(256)}, u32[]{:S(2)}) copy-start(s32[256]{0:T(256)} %param.9) | copy-start | bytes 3076
  54.9 154.0 %reduce-scatter.3.cloned.1.call-start = ((), (), s32[]{:S(2)}) async-start(), calls=%async_computation.6 | async-start | bytes 1310720 | tf_op jit(solution)/shard_map/reduce_scatter | solution.py:88
  132.3 97.1 %all-gather.9.cloned.1.call-start = ((), (), s32[]{:S(2)}) async-start(), calls=%async_computation.9 | async-start | bytes 1310720 | tf_op jit(solution)/shard_map/all_gather | solution.py:110
  164.1 107.5 %all-gather.11.cloned.1.call-start = ((), (), s32[]{:S(2)}) async-start(), calls=%async_computation.10 | async-start | bytes 4718592 | tf_op jit(solution)/shard_map/all_gather | solution.py:125
  164.7 6.3 %collective-permute-start = (s32[256]{0:T(256)S(1)}, s32[256]{0:T(256)S(1)}, u32[]{:S(2)}, u32[]{:S(2)}) collective-permute-start(s32[256]{0:T(256)S(1)} %copy-done.1), channel_id=1, source_target_pairs={{0,1},{1,2},{2,3},{3,4},{4,5},{5,6},{6,7},{7,0},{8,9},{9,10},{10,1... | collective-permute-start | bytes 3080 | tf_op jit(solution)/shard_map/ppermute | solution.py:100
  171.0 6.3 %collective-permute-start.1 = (s32[256]{0:T(256)S(1)}, s32[256]{0:T(256)S(1)}, u32[]{:S(2)}, u32[]{:S(2)}) collective-permute-start(s32[256]{0:T(256)S(1)} %collective-permute-done), channel_id=1, source_target_pairs={{0,1},{1,2},{2,3},{3,4},{4,5},{5,6},{6,7},{7,0},{8,9},{9,10},{10,1... | collective-permute-start | bytes 3080 | tf_op jit(solution)/shard_map/ppermute | solution.py:100
  177.3 6.3 %collective-permute-start.2 = (s32[256]{0:T(256)S(1)}, s32[256]{0:T(256)S(1)}, u32[]{:S(2)}, u32[]{:S(2)}) collective-permute-start(s32[256]{0:T(256)S(1)} %collective-permute-done.1), channel_id=1, source_target_pairs={{0,1},{1,2},{2,3},{3,4},{4,5},{5,6},{6,7},{7,0},{8,9},{9,10},{10,1... | collective-permute-start | bytes 3080 | tf_op jit(solution)/shard_map/ppermute | solution.py:100
  183.5 6.3 %collective-permute-start.3 = (s32[256]{0:T(256)S(1)}, s32[256]{0:T(256)S(1)}, u32[]{:S(2)}, u32[]{:S(2)}) collective-permute-start(s32[256]{0:T(256)S(1)} %collective-permute-done.2), channel_id=1, source_target_pairs={{0,1},{1,2},{2,3},{3,4},{4,5},{5,6},{6,7},{7,0},{8,9},{9,10},{10,1... | collective-permute-start | bytes 3080 | tf_op jit(solution)/shard_map/ppermute | solution.py:100
  189.8 6.3 %collective-permute-start.4 = (s32[256]{0:T(256)S(1)}, s32[256]{0:T(256)S(1)}, u32[]{:S(2)}, u32[]{:S(2)}) collective-permute-start(s32[256]{0:T(256)S(1)} %collective-permute-done.3), channel_id=1, source_target_pairs={{0,1},{1,2},{2,3},{3,4},{4,5},{5,6},{6,7},{7,0},{8,9},{9,10},{10,1... | collective-permute-start | bytes 3080 | tf_op jit(solution)/shard_map/ppermute | solution.py:100
  196.1 6.3 %collective-permute-start.5 = (s32[256]{0:T(256)S(1)}, s32[256]{0:T(256)S(1)}, u32[]{:S(2)}, u32[]{:S(2)}) collective-permute-start(s32[256]{0:T(256)S(1)} %collective-permute-done.4), channel_id=1, source_target_pairs={{0,1},{1,2},{2,3},{3,4},{4,5},{5,6},{6,7},{7,0},{8,9},{9,10},{10,1... | collective-permute-start | bytes 3080 | tf_op jit(solution)/shard_map/ppermute | solution.py:100
  202.4 6.4 %collective-permute-start.6 = (s32[256]{0:T(256)S(1)}, s32[256]{0:T(256)S(1)}, u32[]{:S(2)}, u32[]{:S(2)}) collective-permute-start(s32[256]{0:T(256)S(1)} %collective-permute-done.5), channel_id=1, source_target_pairs={{0,1},{1,2},{2,3},{3,4},{4,5},{5,6},{6,7},{7,0},{8,9},{9,10},{10,1... | collective-permute-start | bytes 3080 | tf_op jit(solution)/shard_map/ppermute | solution.py:100
  210.9 18.5 %all-to-all-start = ((bf16[64,8,128]{2,0,1:T(8,128)(2,1)}), bf16[64,8,128]{2,0,1:T(8,128)(2,1)S(1)}, u32[]{:S(2)}, u32[]{:S(2)}) async-start(bf16[64,8,128]{2,0,1:T(8,128)(2,1)} %pad_maximum_fusion), calls=%async_computation.1 | async-start | bytes 262144 | tf_op jit(solution)/shard_map/all_to_all | solution.py:95
  229.4 4.1 %copy-start.2 = (bf16[2048,256]{1,0:T(8,128)(2,1)S(1)}, bf16[2048,256]{1,0:T(8,128)(2,1)}, u32[]{:S(2)}) copy-start(bf16[2048,256]{1,0:T(8,128)(2,1)} %all-gather.9.cloned.1.call-done) | copy-start | bytes 3145732
Sparse Core Ops, SparseCore 0:
  9.5 42.9 all-gather.6
  54.5 73.3 all-gather.4
  130.4 18.2 reduce-scatter.4
  151.1 24.8 reduce-scatter.2
  177.3 16.7 all-gather.8
  196.1 75.4 all-gather.10
